TPU v7x, 32 devices: a whole 2x2x4 slice. The times are simulated.
32 devices in a mesh: dp: 8 (over y, x, core), mp: 4 (over z).
Axes of the slice: x: 2, y: 2, z: 4, core: 2. Of those that a mesh axis runs over, the one named last changes fastest.
Arguments:
- token_ids: int32 [16], replicated, may hold values from 0 to 3071
- cache_lengths: int32 [16], P('dp'), may hold values from 1 to 512
- embedding: bfloat16 [3072, 12288], P(('dp', 'mp')), may hold values from -6 to 6
- ln_gain: float32 [12288], replicated, may hold values from 0.25 to 1.75
- query_weight: bfloat16 [12288, 6144], P('dp', 'mp'), may hold values from -0.0546875 to 0.0546875
- key_cache: bfloat16 [16, 512, 6144], P('dp', None, 'mp'), may hold values from -1000 to 1000
- value_cache: bfloat16 [16, 512, 6144], P('dp', None, 'mp'), may hold values from -6 to 6
- out_weight: bfloat16 [6144, 12288], P('mp', 'dp'), may hold values from -0.078125 to 0.078125
- final_gain: float32 [12288], replicated, may hold values from 0.25 to 1.75
Outputs:
- log_probs: float32 [16, 3072], P(None, ('dp', 'mp'))
All inputs are finite; a program needn't handle non-finite values.
Results may differ from a plain program's by a relative error of at most 0.00033.
Values may be sent and summed in bfloat16 or wider, within the bound.
A program may use at most 128 MiB of HBM per device.

v0:
```python
import jax
import jax.numpy as jnp
from jax import lax
from jax.sharding import PartitionSpec as P

HD = 128


def per_device(
    token_ids,
    cache_lengths,
    embedding,
    ln_gain,
    query_weight,
    key_cache,
    value_cache,
    out_weight,
    final_gain,
):
    voc_rows = embedding.shape[0]
    model_width = embedding.shape[1]
    vocab_start = lax.axis_index(("dp", "mp")) * voc_rows
    one_hot = (token_ids[:, None] - vocab_start == jnp.arange(voc_rows)[None, :]).astype(
        jnp.bfloat16
    )
    partial_rows = jnp.dot(one_hot, embedding, preferred_element_type=jnp.float32)
    seq_here = key_cache.shape[0]
    cache_len = key_cache.shape[1]
    cols_here = out_weight.shape[1]
    dp_index = lax.axis_index("dp")
    block_sums = lax.psum_scatter(
        partial_rows.astype(jnp.bfloat16), "dp", scatter_dimension=1, tiled=True
    )
    embedded_cols = lax.psum(block_sums, "mp").astype(jnp.float32)
    first_sum, first_sq = lax.psum(
        (jnp.sum(embedded_cols, axis=-1), jnp.sum(embedded_cols * embedded_cols, axis=-1)), "dp"
    )
    first_mean = first_sum / model_width
    first_var = first_sq / model_width - first_mean * first_mean
    ln_here = lax.dynamic_slice_in_dim(ln_gain, dp_index * cols_here, cols_here, 0)
    normed_cols = (
        ln_here * (embedded_cols - first_mean[:, None]) * lax.rsqrt(first_var[:, None] + 1e-05)
    ).astype(jnp.bfloat16)
    own_rows = lax.all_to_all(normed_cols, "dp", split_axis=0, concat_axis=1, tiled=True)
    query_sum = jnp.dot(
        own_rows,
        lax.all_gather(query_weight, "dp", axis=0, tiled=True),
        preferred_element_type=jnp.float32,
    )
    queries = (query_sum * HD ** (-0.5)).astype(jnp.bfloat16)
    heads_here = queries.shape[1] // HD
    head_query = queries.reshape(seq_here, heads_here, HD)
    key_heads = key_cache.reshape(seq_here, cache_len, heads_here, HD)
    value_heads = value_cache.reshape(seq_here, cache_len, heads_here, HD)
    scores = jnp.einsum("shd,sthd->sht", head_query, key_heads, preferred_element_type=jnp.float32)
    live_mask = jnp.arange(cache_len)[None, None, :] < cache_lengths[:, None, None]
    scores = jnp.where(live_mask, scores, jnp.float32(-1e30))
    row_top = jnp.max(scores, axis=-1, keepdims=True)
    exp_terms = jnp.exp(scores - row_top)
    weights = (exp_terms / jnp.sum(exp_terms, axis=-1, keepdims=True)).astype(jnp.bfloat16)
    attended = jnp.einsum("sht,sthd->shd", weights, value_heads, preferred_element_type=jnp.float32)
    attended = attended.astype(jnp.bfloat16).reshape(seq_here, heads_here * HD)
    every_seq = lax.all_gather(attended, "dp", axis=0, tiled=True)
    mixed_out = lax.psum(jnp.dot(every_seq, out_weight, preferred_element_type=jnp.float32), "mp")
    hidden = embedded_cols + mixed_out
    row_sum, row_sq = lax.psum((jnp.sum(hidden, axis=-1), jnp.sum(hidden * hidden, axis=-1)), "dp")
    row_mean = row_sum / model_width
    row_var = row_sq / model_width - row_mean * row_mean
    gain_here = lax.dynamic_slice_in_dim(final_gain, dp_index * cols_here, cols_here, 0)
    final_normed = (
        gain_here * (hidden - row_mean[:, None]) * lax.rsqrt(row_var[:, None] + 1e-05)
    ).astype(jnp.bfloat16)
    logits = lax.dot_general(
        lax.all_gather(final_normed, "dp", axis=1, tiled=True),
        embedding,
        (((1,), (1,)), ((), ())),
        preferred_element_type=jnp.float32,
    )
    local_top = jnp.max(logits, axis=-1)
    global_top = lax.pmax(local_top, ("dp", "mp"))
    total_exp = lax.psum(jnp.sum(jnp.exp(logits - global_top[:, None]), axis=-1), ("dp", "mp"))
    return logits - global_top[:, None] - jnp.log(total_exp)[:, None]


def solution(mesh):
    return jax.shard_map(
        per_device,
        mesh=mesh,
        in_specs=(
            P(),
            P("dp"),
            P(("dp", "mp"), None),
            P(),
            P("dp", "mp"),
            P("dp", None, "mp"),
            P("dp", None, "mp"),
            P("mp", "dp"),
            P(),
        ),
        out_specs=P(None, ("dp", "mp")),
        check_vma=False,
    )
```

profile of v0, /device:TPU:0, one launch (start us, length us, event | category | flops | bytes accessed | tf_op | source)
XLA Modules:
  0.0 406.1 jit_solution(14732259672830846114)
XLA Ops:
  6.5 0.8 broadcast_subtract_fusion
  7.3 0.9 copy-done
  8.2 1.2 convolution_convert_fusion
  11.0 36.0 %reduce-scatter.2.cloned.1.call-done = bf16[16,1536]{1,0:T(8,128)(2,1)} async-done(((bf16[16,12288]{1,0:T(8,128)(2,1)}), bf16[16,1536]{1,0:T(8,128)(2,1)}) %reduce-scatter.2.cloned.1.call-update) | async-done | bytes 49168 | tf_op jit(solution)/shard_map/reduce_scatter | solution.py:31
  47.0 19.9 %psum.49 = bf16[16,1536]{1,0:T(8,128)(2,1)S(1)} all-reduce(bf16[16,1536]{1,0:T(8,128)(2,1)} %reduce-scatter.2.cloned.1.call-done), channel_id=1, replica_groups=mesh['dp'=8,'mp'=4] {'mp'}, use_global_device_ids=true, to_apply=%region_1.0 | all-reduce | flops 24576 | bytes 98304 | tf_op jit(solution)/shard_map/psum | solution.py:34
  67.1 12.8 %all-reduce.1 = (f32[16]{0:T(128)S(1)}, f32[16]{0:T(128)S(1)}) all-reduce(f32[16]{0:T(128)S(1)} %get-tuple-element.8, f32[16]{0:T(128)S(1)} %get-tuple-element.7), channel_id=1, replica_groups=mesh['dp'=8,'mp'=4] {'dp'}, use_global_device_ids=true, to_apply=%region_5.0 | all-reduce | flops 32 | bytes 256 | tf_op jit(solution)/shard_map/psum | solution.py:35
  80.6 3.3 all-to-all-start
  84.1 4.7 %copy.14 = bf16[2,512,1536]{1,2,0:T(8,128)(2,1)} copy(bf16[2,512,1536]{2,1,0:T(8,128)(2,1)} %param.14) | data formatting | bytes 6291456 | tf_op args[5]
  88.8 4.7 %copy.15 = bf16[2,512,1536]{1,2,0:T(8,128)(2,1)} copy(bf16[2,512,1536]{2,1,0:T(8,128)(2,1)} %param.15) | data formatting | bytes 6291456 | tf_op args[6]
  93.4 135.6 %all-gather.3.cloned.1.call-done = bf16[12288,1536]{1,0:T(8,128)(2,1)} async-done(((bf16[1536,1536]{1,0:T(8,128)(2,1)}), bf16[12288,1536]{1,0:T(8,128)(2,1)}) %all-gather.3.cloned.1.call-update) | async-done | bytes 37748752 | tf_op jit(solution)/shard_map/all_gather | solution.py:47
  229.1 14.3 %fusion.2 = bf16[2,1536]{1,0:T(2,128)(2,1)S(1)} fusion(bf16[2,12288]{1,0:T(2,128)(2,1)S(1)} %bitcast.29, bf16[12288,1536]{1,0:T(8,128)(2,1)} %all-gather.3.cloned.1.call-done), kind=kOutput, calls=%fused_computation.4 | convolution fusion | flops 75503616 | bytes 37804032 | tf_op jit(solution)/shard_map/dot_general | solution.py:45
  243.4 2.4 fusion.20
  246.0 2.8 fusion.12
  248.8 9.1 %all-gather = bf16[8,2,1536]{2,1,0:T(2,128)(2,1)S(1)} all-gather(bf16[1,2,1536]{2,1,0:T(2,128)(2,1)S(1)} %reshape.56), channel_id=1, replica_groups=mesh['dp'=8,'mp'=4] {'dp'}, dimensions={0}, use_global_device_ids=true | all-gather | bytes 55296 | tf_op jit(solution)/shard_map/all_gather | solution.py:63
  258.0 3.7 fusion.21
  261.7 0.8 dynamic_slice.6
  262.5 33.8 %all-reduce.4.cloned.1.call-done = f32[16,1536]{1,0:T(8,128)} async-done(((f32[16,1536]{1,0:T(8,128)}), f32[16,1536]{1,0:T(8,128)}) %all-reduce.4.cloned.1.call-update) | async-done | bytes 98320 | tf_op jit(solution)/shard_map/psum | solution.py:64
  296.3 1.0 fusion.14
  297.3 11.8 %all-reduce = (f32[16]{0:T(128)S(1)}, f32[16]{0:T(128)S(1)}) all-reduce(f32[16]{0:T(128)S(1)} %get-tuple-element.6, f32[16]{0:T(128)S(1)} %get-tuple-element.5), channel_id=1, replica_groups=mesh['dp'=8,'mp'=4] {'dp'}, use_global_device_ids=true, to_apply=%region_12.13 | all-reduce | flops 32 | bytes 256 | tf_op jit(solution)/shard_map/psum | solution.py:66
  309.2 1.0 multiply_convert_fusion
  310.1 9.5 %all_gather.11 = bf16[16,12288]{1,0:T(8,128)(2,1)S(1)} all-gather(bf16[16,1536]{1,0:T(8,128)(2,1)S(1)} %multiply_convert_fusion), channel_id=1, replica_groups=mesh['dp'=8,'mp'=4] {'dp'}, dimensions={1}, use_global_device_ids=true | all-gather | bytes 442368 | tf_op jit(solution)/shard_map/all_gather | solution.py:74
  319.7 0.8 fusion.19
  320.5 39.2 %pmax.7 = f32[16]{0:T(128)S(1)} all-reduce(f32[16]{0:T(128)S(1)} %get-tuple-element.17), channel_id=1, replica_groups=mesh['dp'=8,'mp'=4] {'dp','mp'}, use_global_device_ids=true, to_apply=%region_14.15 | all-reduce | flops 16 | bytes 128 | tf_op jit(solution)/shard_map/pmax | solution.py:80
  359.9 39.0 %psum.55 = f32[16]{0:T(128)S(1)} all-reduce(f32[16]{0:T(128)S(1)} %exponential_reduce_fusion), channel_id=1, replica_groups=mesh['dp'=8,'mp'=4] {'dp','mp'}, use_global_device_ids=true, to_apply=%region_16.17 | all-reduce | flops 16 | bytes 128 | tf_op jit(solution)/shard_map/psum | solution.py:81
  (25 shorter events, 3.7 us)
Async XLA Ops:
  6.5 1.7 copy-start
  6.5 40.5 %reduce-scatter.2.cloned.1.call-start = ((), (), s32[]{:S(2)}) async-start(), calls=%async_computation.2 | async-start | bytes 442368 | tf_op jit(solution)/shard_map/reduce_scatter | solution.py:31
  9.5 74.5 %copy-start.1 = (s32[2]{0:T(128)S(1)}, s32[2]{0:T(128)}, u32[]{:S(2)}) copy-start(s32[2]{0:T(128)} %param.10) | copy-start | bytes 28
  9.5 219.6 %all-gather.3.cloned.1.call-start = ((), (), s32[]{:S(2)}) async-start(), calls=%async_computation.3 | async-start | bytes 42467328 | tf_op jit(solution)/shard_map/all_gather | solution.py:47
  80.6 12.9 %all-to-all-start = ((bf16[8,2,1536]{2,1,0:T(2,128)(2,1)}), bf16[8,2,1536]{2,1,0:T(2,128)(2,1)S(1)}, u32[]{:S(2)}, u32[]{:S(2)}) async-start(bf16[8,2,1536]{2,1,0:T(2,128)(2,1)} %all_to_all.14), calls=%async_computation.1 | async-start | bytes 98304 | tf_op jit(solution)/shard_map/all_to_all | solution.py:44
  83.9 212.4 %all-reduce.4.cloned.1.call-start = ((), (), s32[]{:S(2)}) async-start(), calls=%async_computation.4 | async-start | bytes 196608 | tf_op jit(solution)/shard_map/psum | solution.py:64
Sparse Core Ops, SparseCore 0:
  10.4 36.5 reduce-scatter.1
  48.9 180.1 all-gather.2
  261.8 34.4 all-reduce.3
where the time goes:
time: 407 us; the launch traced here: 406 us
  waiting for transfers between devices  206 us (51%)
  blocking collectives  141 us (35%)
  matrix products  25.2 us (6%)
  between operations  13.2 us (3%)
  local copies, waits for them, and re-layouts  12.6 us (3%)
  other arithmetic  4.18 us (1%)
    all_gather x1, waiting for transfers between devices, per_device(): lax.all_gather(query_weight, 'dp', axis=0, tiled=True)  136 us
    pmax x1, blocking collectives, per_device(): global_top = lax.pmax(local_top, ('dp', 'mp'))  39.2 us
    psum x1, blocking collectives, per_device(): lax.psum(jnp.sum(jnp.exp(logits - global_top[:, None]), axis=-1), ('dp',...  39 us
    reduce_scatter x1, waiting for transfers between devices, per_device(): lax.psum_scatter(partial_rows.astype(jnp.bfloat16), 'dp', scatter_dimensi...  36 us
    psum x1, waiting for transfers between devices, per_device(): lax.psum(jnp.dot(every_seq, out_weight, preferred_element_type=jnp.float3...  33.8 us
    psum x1, blocking collectives, per_device(): embedded_cols = lax.psum(block_sums, 'mp').astype(jnp.float32)  19.9 us
    dot_general x1, matrix products, per_device(): jnp.dot(own_rows, lax.all_gather(query_weight, 'dp', axis=0, tiled=True),...  14.3 us
    psum x1, blocking collectives, per_device(): lax.psum((jnp.sum(embedded_cols, axis=-1), jnp.sum(embedded_cols * embedd...  12.8 us
  transfers between devices with their start and end apart: 4, of which 3 were waited for; matrix products, arithmetic and copies ran while one was open for 3% of the time, Pallas kernels for 0%

commit v1 on v0

--- a/solution.py
+++ b/solution.py
@@ -61,7 +61,8 @@
     attended = jnp.einsum("sht,sthd->shd", weights, value_heads, preferred_element_type=jnp.float32)
     attended = attended.astype(jnp.bfloat16).reshape(seq_here, heads_here * HD)
     every_seq = lax.all_gather(attended, "dp", axis=0, tiled=True)
-    mixed_out = lax.psum(jnp.dot(every_seq, out_weight, preferred_element_type=jnp.float32), "mp")
+    m = jnp.dot(every_seq, out_weight, preferred_element_type=jnp.float32)
+    mixed_out = lax.all_gather(m, "mp").sum(axis=0)
     hidden = embedded_cols + mixed_out
     row_sum, row_sq = lax.psum((jnp.sum(hidden, axis=-1), jnp.sum(hidden * hidden, axis=-1)), "dp")
     row_mean = row_sum / model_width

time: 407 us -> 387 us (0.951)
  waiting for transfers between devices: 206 us -> 172 us
  blocking collectives: 141 us -> 158 us
    psum x1 -> x0, waiting for transfers between devices: 33.8 us -> none  [per_device(): lax.psum(jnp.dot(every_seq, out_weight, preferred_element_type=jnp.float3...]
    all_gather x0 -> x1, blocking collectives: none -> 14.7 us  [per_device(): mixed_out = lax.all_gather(m, 'mp').sum(axis=0)]
  transfers between devices with their start and end apart: 4 -> 3, of which waited for: 3 -> 2; matrix products, arithmetic and copies ran while one was open for 3% -> 3% of each run, Pallas kernels for 0% -> 0%
where the time goes in v1:
time: 387 us; the launch traced here: 386 us
  waiting for transfers between devices  172 us (44%)
  blocking collectives  158 us (41%)
  matrix products  24.6 us (6%)
  between operations  13.5 us (3%)
  local copies, waits for them, and re-layouts  12.5 us (3%)
    all_gather x1, waiting for transfers between devices, per_device(): lax.all_gather(query_weight, 'dp', axis=0, tiled=True)  135 us
    psum x1, blocking collectives, per_device(): lax.psum(jnp.sum(jnp.exp(logits - global_top[:, None]), axis=-1), ('dp',...  41.1 us
    pmax x1, blocking collectives, per_device(): global_top = lax.pmax(local_top, ('dp', 'mp'))  39.9 us
    reduce_scatter x1, waiting for transfers between devices, per_device(): lax.psum_scatter(partial_rows.astype(jnp.bfloat16), 'dp', scatter_dimensi...  36 us
    psum x1, blocking collectives, per_device(): embedded_cols = lax.psum(block_sums, 'mp').astype(jnp.float32)  19.9 us
    all_gather x1, blocking collectives, per_device(): mixed_out = lax.all_gather(m, 'mp').sum(axis=0)  14.7 us
    dot_general x1, matrix products, per_device(): jnp.dot(own_rows, lax.all_gather(query_weight, 'dp', axis=0, tiled=True),...  14.3 us
    psum x1, blocking collectives, per_device(): lax.psum((jnp.sum(embedded_cols, axis=-1), jnp.sum(embedded_cols * embedd...  12.8 us
  transfers between devices with their start and end apart: 3, of which 2 were waited for; matrix products, arithmetic and copies ran while one was open for 3% of the time, Pallas kernels for 0%

profile of v1, /device:TPU:0, one launch (start us, length us, event | category | flops | bytes accessed | tf_op | source)
XLA Modules:
  0.0 386.0 jit_solution(8414278317100146004)
XLA Ops:
  6.5 0.8 broadcast_subtract_fusion
  7.3 0.9 copy-done
  8.2 1.2 convolution_convert_fusion
  9.5 0.7 all-gather.4.cloned.1.call-update
  10.2 0.8 dynamic_slice.7
  11.0 36.0 %reduce-scatter.2.cloned.1.call-done = bf16[16,1536]{1,0:T(8,128)(2,1)} async-done(((bf16[16,12288]{1,0:T(8,128)(2,1)}), bf16[16,1536]{1,0:T(8,128)(2,1)}) %reduce-scatter.2.cloned.1.call-update) | async-done | bytes 49168 | tf_op jit(solution)/shard_map/reduce_scatter | solution.py:31
  47.0 19.9 %psum.42 = bf16[16,1536]{1,0:T(8,128)(2,1)S(1)} all-reduce(bf16[16,1536]{1,0:T(8,128)(2,1)} %reduce-scatter.2.cloned.1.call-done), channel_id=1, replica_groups=mesh['dp'=8,'mp'=4] {'mp'}, use_global_device_ids=true, to_apply=%region_1.0 | all-reduce | flops 24576 | bytes 98304 | tf_op jit(solution)/shard_map/psum | solution.py:34
  67.1 12.8 %all-reduce.1 = (f32[16]{0:T(128)S(1)}, f32[16]{0:T(128)S(1)}) all-reduce(f32[16]{0:T(128)S(1)} %get-tuple-element.8, f32[16]{0:T(128)S(1)} %get-tuple-element.7), channel_id=1, replica_groups=mesh['dp'=8,'mp'=4] {'dp'}, use_global_device_ids=true, to_apply=%region_5.0 | all-reduce | flops 32 | bytes 256 | tf_op jit(solution)/shard_map/psum | solution.py:35
  80.6 3.3 all-to-all-start
  84.0 4.7 %copy.14 = bf16[2,512,1536]{1,2,0:T(8,128)(2,1)} copy(bf16[2,512,1536]{2,1,0:T(8,128)(2,1)} %param.14) | data formatting | bytes 6291456 | tf_op args[5]
  88.7 4.7 %copy.15 = bf16[2,512,1536]{1,2,0:T(8,128)(2,1)} copy(bf16[2,512,1536]{2,1,0:T(8,128)(2,1)} %param.15) | data formatting | bytes 6291456 | tf_op args[6]
  93.4 0.8 dynamic_slice.6
  94.2 134.9 %all-gather.4.cloned.1.call-done = bf16[12288,1536]{1,0:T(8,128)(2,1)} async-done(((bf16[1536,1536]{1,0:T(8,128)(2,1)}), bf16[12288,1536]{1,0:T(8,128)(2,1)}) %all-gather.4.cloned.1.call-update) | async-done | bytes 37748752 | tf_op jit(solution)/shard_map/all_gather | solution.py:47
  229.1 14.3 %fusion.2 = bf16[2,1536]{1,0:T(2,128)(2,1)S(1)} fusion(bf16[2,12288]{1,0:T(2,128)(2,1)S(1)} %bitcast.31, bf16[12288,1536]{1,0:T(8,128)(2,1)} %all-gather.4.cloned.1.call-done), kind=kOutput, calls=%fused_computation.4 | convolution fusion | flops 75503616 | bytes 37804032 | tf_op jit(solution)/shard_map/dot_general | solution.py:45
  243.4 2.4 fusion.20
  246.0 2.8 fusion.12
  248.8 9.1 %all-gather.1 = bf16[8,2,1536]{2,1,0:T(2,128)(2,1)S(1)} all-gather(bf16[1,2,1536]{2,1,0:T(2,128)(2,1)S(1)} %reshape.57), channel_id=1, replica_groups=mesh['dp'=8,'mp'=4] {'dp'}, dimensions={0}, use_global_device_ids=true | all-gather | bytes 55296 | tf_op jit(solution)/shard_map/all_gather | solution.py:63
  258.0 3.1 fusion.21
  261.0 14.7 %all-gather = f32[64,1536]{1,0:T(8,128)S(1)} all-gather(f32[16,1536]{1,0:T(8,128)S(1)} %fusion.21), channel_id=2, replica_groups=mesh['dp'=8,'mp'=4] {'mp'}, dimensions={0}, use_global_device_ids=true | all-gather | bytes 491520 | tf_op jit(solution)/shard_map/all_gather | solution.py:65
  275.9 11.8 %all-reduce = (f32[16]{0:T(128)S(1)}, f32[16]{0:T(128)S(1)}) all-reduce(f32[16]{0:T(128)S(1)} %get-tuple-element.6, f32[16]{0:T(128)S(1)} %get-tuple-element.5), channel_id=1, replica_groups=mesh['dp'=8,'mp'=4] {'dp'}, use_global_device_ids=true, to_apply=%region_12.13 | all-reduce | flops 32 | bytes 256 | tf_op jit(solution)/shard_map/psum | solution.py:67
  287.9 8.6 %all_gather.19 = bf16[16,12288]{1,0:T(8,128)(2,1)S(1)} all-gather(bf16[16,1536]{1,0:T(8,128)(2,1)S(1)} %multiply_convert_fusion), channel_id=1, replica_groups=mesh['dp'=8,'mp'=4] {'dp'}, dimensions={1}, use_global_device_ids=true | all-gather | bytes 442368 | tf_op jit(solution)/shard_map/all_gather | solution.py:75
  296.5 0.8 fusion.19
  297.3 39.9 %pmax.7 = f32[16]{0:T(128)S(1)} all-reduce(f32[16]{0:T(128)S(1)} %get-tuple-element.17), channel_id=1, replica_groups=mesh['dp'=8,'mp'=4] {'dp','mp'}, use_global_device_ids=true, to_apply=%region_14.15 | all-reduce | flops 16 | bytes 128 | tf_op jit(solution)/shard_map/pmax | solution.py:81
  337.4 41.1 %psum.47 = f32[16]{0:T(128)S(1)} all-reduce(f32[16]{0:T(128)S(1)} %exponential_reduce_fusion), channel_id=1, replica_groups=mesh['dp'=8,'mp'=4] {'dp','mp'}, use_global_device_ids=true, to_apply=%region_16.17 | all-reduce | flops 16 | bytes 128 | tf_op jit(solution)/shard_map/psum | solution.py:82
  (24 shorter events, 2.4 us)
Async XLA Ops:
  6.5 1.7 copy-start
  6.5 40.5 %reduce-scatter.2.cloned.1.call-start = ((), (), s32[]{:S(2)}) async-start(), calls=%async_computation.2 | async-start | bytes 442368 | tf_op jit(solution)/shard_map/reduce_scatter | solution.py:31
  9.5 74.5 %copy-start.1 = (s32[2]{0:T(128)S(1)}, s32[2]{0:T(128)}, u32[]{:S(2)}) copy-start(s32[2]{0:T(128)} %param.10) | copy-start | bytes 28
  9.5 219.6 %all-gather.4.cloned.1.call-start = ((), (), s32[]{:S(2)}) async-start(), calls=%async_computation.3 | async-start | bytes 42467328 | tf_op jit(solution)/shard_map/all_gather | solution.py:47
  80.6 13.6 %all-to-all-start = ((bf16[8,2,1536]{2,1,0:T(2,128)(2,1)}), bf16[8,2,1536]{2,1,0:T(2,128)(2,1)S(1)}, u32[]{:S(2)}, u32[]{:S(2)}) async-start(bf16[8,2,1536]{2,1,0:T(2,128)(2,1)} %all_to_all.14), calls=%async_computation.1 | async-start | bytes 98304 | tf_op jit(solution)/shard_map/all_to_all | solution.py:44
Sparse Core Ops, SparseCore 0:
  10.4 36.5 reduce-scatter.1
  48.9 180.1 all-gather.3
